TPU v7x, 32 devices: a whole 2x2x4 slice. The times are simulated.
32 devices in a mesh: head: 4 (over x, core), ctx: 8 (over z, y).
Axes of the slice: x: 2, y: 2, z: 4, core: 2. Of those that a mesh axis runs over, the one named last changes fastest.
Arguments:
- token_ids: int32 [2, 16], replicated, may hold values from 0 to 64127
- suffix_lengths: int32 [16], replicated, may hold values from 0 to 128, as said below
- embedding: bfloat16 [64128, 16384], P('ctx', 'head'), may hold values from -36 to 36
- attn_gain: float32 [16384], P('head'), may hold values from 0.25 to 1.75
- qkv_weight: bfloat16 [16384, 8, 1280], P('head', None, 'ctx'), may hold values from -0.046875 to 0.046875
- out_weight: bfloat16 [8192, 16384], P('head', 'ctx'), may hold values from -0.0625 to 0.0625
- prefix_keys: bfloat16 [8, 32768, 128], P('head', 'ctx'), may hold values from -32 to 32
- prefix_values: bfloat16 [8, 32768, 128], P('head', 'ctx'), may hold values from -8 to 8
- suffix_keys: bfloat16 [16, 128, 8, 128], P('ctx', None, 'head'), may hold values from -32 to 32
- suffix_values: bfloat16 [16, 128, 8, 128], P('ctx', None, 'head'), may hold values from -12 to 12
Outputs:
- attn_out: bfloat16 [16, 2, 16384], P('head', None, 'ctx')
Inputs may be any that keep to these rules, and one draw needn't show every extreme that they name: Sequence b's suffix cache holds its tokens in slots 0 .. suffix_lengths[b] - 1; some sequence fills all 128 slots.
All inputs are finite; a program needn't handle non-finite values.
Results may differ from a plain program's by a relative error of at most 0.02.
Values may be sent and summed in bfloat16 or wider, within the bound.
No kernel may reach another device: no remote copies, remote signals or barrier semaphores. Data moves between devices by JAX's collectives and lax.ppermute only.
A program may use at most 128 MiB of HBM per device.

v0:
```python
import jax
import jax.numpy as jnp
from jax import lax
from jax.sharding import PartitionSpec as P

EPSILON = 1e-05
ROTARY_THETA = 500000.0
MASKED = -1e30


def combined_all(part, axis, combine):
    gathered = jax.tree.map(lambda a: lax.all_gather(a, axis), part)

    def take(source):
        return jax.tree.map(lambda a: lax.dynamic_index_in_dim(a, source, 0, False), gathered)

    return lax.fori_loop(
        1, lax.axis_size(axis), lambda source, state: combine(state, take(source)), take(0)
    )


def rotary(vectors, positions):
    half_width = vectors.shape[-1] // 2
    frequency = ROTARY_THETA ** (
        -2.0 * jnp.arange(half_width).astype(jnp.float32) / vectors.shape[-1]
    )
    angles = positions[..., None] * frequency
    cosine = jnp.cos(angles)
    sine_values = jnp.sin(angles)
    front_half = vectors[..., :half_width]
    back_half = vectors[..., half_width:]
    return jnp.concatenate(
        [
            front_half * cosine - back_half * sine_values,
            back_half * cosine + front_half * sine_values,
        ],
        axis=-1,
    )


def combine(earlier, later):
    highest = jnp.maximum(earlier[0], later[0])
    first_scale = jnp.exp(earlier[0] - highest)
    second_scale = jnp.exp(later[0] - highest)
    return (
        highest,
        earlier[1] * first_scale + later[1] * second_scale,
        earlier[2] * first_scale[..., None] + later[2] * second_scale[..., None],
    )


def weigh_scores(scores):
    maxima = jnp.max(scores, axis=-1)
    weights = jnp.exp(scores - maxima[..., None]).astype(jnp.bfloat16)
    return (maxima, weights, jnp.sum(weights.astype(jnp.float32), axis=-1))


def lookup_rows(step_tokens, embedding):
    local_rows = embedding.shape[0]
    offsets = step_tokens - lax.axis_index("ctx") * local_rows
    inside_range = (offsets >= 0) & (offsets < local_rows)
    picked = jnp.take(embedding, jnp.clip(offsets, 0, local_rows - 1), axis=0)
    picked = jnp.where(inside_range[..., None], picked, jnp.zeros((), jnp.bfloat16))
    return lax.psum(picked, "ctx").astype(jnp.float32).astype(jnp.bfloat16)


def project(embedded, attn_gain, qkv_weight):
    features = embedded.astype(jnp.float32)
    square_sum = lax.psum(jnp.sum(features * features, axis=-1), "head")
    model_width = features.shape[-1] * lax.axis_size("head")
    normed = (
        features * lax.rsqrt(square_sum / model_width + EPSILON)[..., None] * attn_gain
    ).astype(jnp.bfloat16)
    flattened_rows = normed.reshape(-1, normed.shape[-1])
    local_heads = qkv_weight.shape[1] // lax.axis_size("head")

    def partial_summand(start, count):
        return jnp.einsum(
            "rd,dgf->grf", flattened_rows, qkv_weight, preferred_element_type=jnp.float32
        )

    summed = lax.psum_scatter(
        partial_summand(jnp.int32(0), lax.axis_size("head") * local_heads),
        "head",
        scatter_dimension=0,
        tiled=True,
    )
    return lax.all_gather(summed.astype(jnp.bfloat16), "ctx", axis=2, tiled=True)


def prefix_portion(flat_queries, prefix_keys, prefix_values):

    def one_head(operands):
        queries_block, keys_block, values_block = operands
        scores = jnp.einsum(
            "qd,kd->qk", queries_block, keys_block, preferred_element_type=jnp.float32
        )
        maxima, weights, totals = weigh_scores(scores)
        return (maxima, totals, jnp.dot(weights, values_block, preferred_element_type=jnp.float32))

    return lax.map(one_head, (flat_queries, prefix_keys, prefix_values))


def attend(
    qkv_rows,
    first_step,
    suffix_lengths,
    prefix_keys,
    prefix_values,
    suffix_keys,
    suffix_values,
    seen_keys,
    seen_values,
):
    local_heads, step_count, batch_rows, united_width = qkv_rows.shape
    head_dim = prefix_keys.shape[-1]
    query_width = united_width - 2 * head_dim
    group_size = query_width // head_dim
    queries = qkv_rows[..., :query_width].reshape(
        local_heads, step_count, batch_rows, group_size, head_dim
    )
    new_keys = qkv_rows[..., query_width : query_width + head_dim]
    new_values = qkv_rows[..., query_width + head_dim :]
    context = prefix_keys.shape[1] * lax.axis_size("ctx")
    step_index = first_step + jnp.arange(step_count, dtype=jnp.int32)
    positions = (context + suffix_lengths[None, :] + step_index[:, None]).astype(jnp.float32)
    queries_rot = (
        rotary(queries.astype(jnp.float32), positions[None, :, :, None]) * head_dim ** (-0.5)
    ).astype(jnp.bfloat16)
    keys_rot = rotary(new_keys.astype(jnp.float32), positions[None]).astype(jnp.bfloat16)
    maxima, totals, numerators = prefix_portion(
        queries_rot.reshape(local_heads, -1, head_dim), prefix_keys, prefix_values
    )
    maxima = maxima.reshape(local_heads, step_count, batch_rows, group_size)
    totals = totals.reshape(local_heads, step_count, batch_rows, group_size)
    numerators = numerators.reshape(local_heads, step_count, batch_rows, group_size, head_dim)
    owned_rows = suffix_keys.shape[0]
    own_start = lax.axis_index("ctx") * owned_rows
    own_queries = lax.dynamic_slice_in_dim(queries_rot, own_start, owned_rows, 2)
    own_lengths = lax.dynamic_slice_in_dim(suffix_lengths, own_start, owned_rows, 0)
    seen_keys = jnp.concatenate(
        [seen_keys, lax.dynamic_slice_in_dim(keys_rot, own_start, owned_rows, 2)], axis=1
    )
    seen_values = jnp.concatenate(
        [seen_values, lax.dynamic_slice_in_dim(new_values, own_start, owned_rows, 2)], axis=1
    )
    slot_count = suffix_keys.shape[1]
    near_scores = jnp.einsum(
        "gtbjd,bsgd->gtbjs", own_queries, suffix_keys, preferred_element_type=jnp.float32
    )
    live_slots = jnp.arange(slot_count, dtype=jnp.int32)[None, :] < own_lengths[:, None]
    near_scores = jnp.where(live_slots[None, None, :, None, :], near_scores, MASKED)
    fresh_scores = jnp.einsum(
        "gtbjd,gubd->gtbju", own_queries, seen_keys, preferred_element_type=jnp.float32
    )
    visible = jnp.arange(seen_keys.shape[1], dtype=jnp.int32)[None, :] <= step_index[:, None]
    fresh_scores = jnp.where(visible[None, :, None, None, :], fresh_scores, MASKED)
    nearby_maxima, weights, near_totals = weigh_scores(
        jnp.concatenate([near_scores, fresh_scores], axis=-1)
    )
    near_numerators = jnp.einsum(
        "gtbjs,bsgd->gtbjd",
        weights[..., :slot_count],
        suffix_values,
        preferred_element_type=jnp.float32,
    )
    near_numerators = near_numerators + jnp.einsum(
        "gtbju,gubd->gtbjd",
        weights[..., slot_count:],
        seen_values,
        preferred_element_type=jnp.float32,
    )
    own_part = (
        lax.dynamic_slice_in_dim(maxima, own_start, owned_rows, 2),
        lax.dynamic_slice_in_dim(totals, own_start, owned_rows, 2),
        lax.dynamic_slice_in_dim(numerators, own_start, owned_rows, 2),
    )
    joined = combine(own_part, (nearby_maxima, near_totals, near_numerators))
    maxima = lax.dynamic_update_slice_in_dim(maxima, joined[0], own_start, 2)
    totals = lax.dynamic_update_slice_in_dim(totals, joined[1], own_start, 2)
    numerators = lax.dynamic_update_slice_in_dim(numerators, joined[2], own_start, 2)
    maxima, totals, numerators = combined_all((maxima, totals, numerators), "ctx", combine)
    attention = (numerators / totals[..., None]).astype(jnp.bfloat16)
    return (attention, seen_keys, seen_values)


def project_out(attention, out_weight):
    local_heads, step_count, batch_rows, group_size, head_dim = attention.shape
    flattened_heads = attention.reshape(local_heads, step_count, batch_rows, group_size * head_dim)
    head_weights = out_weight.reshape(local_heads, group_size * head_dim, out_weight.shape[1])
    per_device = batch_rows // lax.axis_size("head")

    def partial_summand(start, count):
        return jnp.einsum(
            "lmie,len->imn", flattened_heads, head_weights, preferred_element_type=jnp.float32
        )

    return lax.psum_scatter(
        partial_summand(jnp.int32(0), lax.axis_size("head") * per_device).astype(jnp.bfloat16),
        "head",
        scatter_dimension=0,
        tiled=True,
    )


def body(
    token_ids,
    suffix_lengths,
    embedding,
    attn_gain,
    qkv_weight,
    out_weight,
    prefix_keys,
    prefix_values,
    suffix_keys,
    suffix_values,
):
    total_steps = token_ids.shape[0]
    batch_rows = token_ids.shape[1]
    local_heads = prefix_keys.shape[0]
    head_dim = prefix_keys.shape[-1]
    step_groups = (0, total_steps)
    seen_keys = jnp.zeros((local_heads, 0, suffix_keys.shape[0], head_dim), jnp.bfloat16)
    seen_values = jnp.zeros((local_heads, 0, suffix_keys.shape[0], head_dim), jnp.bfloat16)
    first_step, step_count = step_groups
    embedded = lookup_rows(token_ids, embedding)
    qkv_rows = project(embedded, attn_gain, qkv_weight)
    qkv_rows = qkv_rows.reshape(local_heads, step_count, batch_rows, qkv_rows.shape[-1])
    attention, seen_keys, seen_values = attend(
        qkv_rows,
        first_step,
        suffix_lengths,
        prefix_keys,
        prefix_values,
        suffix_keys,
        suffix_values,
        seen_keys,
        seen_values,
    )
    results = project_out(attention, out_weight)
    return results


def solution(mesh):
    placed = (
        P(),
        P(),
        P("ctx", "head"),
        P("head"),
        P("head", None, "ctx"),
        P("head", "ctx"),
        P("head", "ctx", None),
        P("head", "ctx", None),
        P("ctx", None, "head", None),
        P("ctx", None, "head", None),
    )
    return jax.shard_map(
        body, mesh=mesh, in_specs=placed, out_specs=P("head", None, "ctx"), check_vma=False
    )
```

profile of v0, /device:TPU:0, one launch (start us, length us, event | category | flops | bytes accessed | tf_op | source)
XLA Modules:
  0.0 286.1 jit_solution(10977653401740873123)
XLA Ops:
  6.5 0.7 compare_and_fusion
  7.3 0.1 reshape.170
  7.4 2.7 gather_fusion
  10.0 0.8 select_select_fusion
  10.9 0.7 broadcast_add_fusion
  11.6 0.7 dynamic_slice.74
  12.3 0.1 iota_compare_fusion.1
  12.4 0.1 add_convert_fusion.1
  12.5 73.2 %all-reduce.4.cloned.1.call-done = bf16[2,16,4096]{2,1,0:T(8,128)(2,1)} async-done(((bf16[2,16,4096]{2,1,0:T(8,128)(2,1)}), bf16[2,16,4096]{2,1,0:T(8,128)(2,1)}) %all-reduce.4.cloned.1.call-update) | async-done | bytes 262160 | tf_op jit(solution)/shard_map/psum | solution.py:64
  85.6 1.1 fusion.21
  86.7 5.7 %psum.15 = f32[2,16]{1,0:T(2,128)S(1)} all-reduce(f32[2,16]{1,0:T(2,128)S(1)} %fusion.21), channel_id=1, replica_groups=mesh['head'=4,'ctx'=8] {'head'}, use_global_device_ids=true, to_apply=%region_2.3 | all-reduce | flops 32 | bytes 256 | tf_op jit(solution)/shard_map/psum | solution.py:69
  92.4 1.1 fusion.23
  93.5 8.1 %convolution_bitcast_fusion.2 = f32[8,32,160]{2,1,0:T(8,128)} fusion(bf16[32,4096,1]{1,0,2:T(8,128)(2,1)S(1)} %bitcast.139, bf16[4096,8,160]{0,2,1:T(8,128)(2,1)} %param.18), kind=kOutput, calls=%fused_computation.25 | convolution fusion | flops 335544320 | bytes 10911744 | tf_op jit(solution)/shard_map/rd,dgf->grf/dot_general | solution.py:78
  101.6 0.3 multiply_cosine_fusion
  101.9 19.3 %reduce-scatter.3.cloned.1.call-done = f32[2,32,160]{2,1,0:T(8,128)} async-done(((f32[8,32,160]{2,1,0:T(8,128)}), f32[2,32,160]{2,1,0:T(8,128)}) %reduce-scatter.3.cloned.1.call-update) | async-done | bytes 40976 | tf_op jit(solution)/shard_map/reduce_scatter | solution.py:82
  121.2 0.8 convert_element_type.73
  122.1 0.1 copy.73
  122.2 32.0 %all_gather.27 = bf16[2,32,1280]{1,0,2:T(2,128)(2,1)S(1)} all-gather(bf16[2,32,160]{1,0,2:T(2,128)(2,1)S(1)} %copy.73), channel_id=1, replica_groups=mesh['head'=4,'ctx'=8] {'ctx'}, dimensions={2}, use_global_device_ids=true | all-gather | bytes 184320 | tf_op jit(solution)/shard_map/all_gather | solution.py:88
  154.2 0.4 copy.74
  154.7 0.1 fusion.42
  155.0 0.1 fusion.31
  155.1 0.1 add_convert_fusion
  155.2 0.1 fusion.24
  155.4 9.6 %while.33 = (s32[]{:T(128)}, f32[2,256]{1,0:T(2,128)S(1)}, f32[2,256]{1,0:T(2,128)S(1)}, f32[2,256,128]{2,1,0:T(8,128)S(1)}, bf16[2,256,128]{2,1,0:T(8,128)(2,1)...) while((s32[]{:T(128)}, f32[2,256]{1,0:T(2,128)S(1)}, ...), condition=%wide.region_7.8_spmd, body=%wide.region_4.7_spmd.sunk | while | flops 542113280 | bytes 14885997 | solution.py:101
  155.4 2.0 fusion.61
  157.5 0.8 convert_reduce_fusion.3
  158.3 1.9 fusion.62
  160.3 2.0 fusion.61
  162.3 0.8 convert_reduce_fusion.3
  163.1 1.9 fusion.62
  165.0 0.1 reshape.162
  165.2 0.1 reshape.163
  165.3 0.2 fusion.44
  165.5 0.3 fusion.45
  165.8 0.2 convert_reduce_fusion.1
  166.0 0.1 convolution_bitcast_fusion.4
  166.2 0.1 fusion.18
  166.3 0.7 copy-done.1
  167.1 0.1 all_gather.28
  167.2 0.1 all_gather.31
  167.4 0.1 copy.86
  167.5 30.8 %all_gather.33 = f32[8,2,2,16,8]{3,4,2,1,0:T(8,128)S(1)} all-gather(f32[1,2,2,16,8]{3,4,2,1,0:T(8,128)S(1)} %copy.86), channel_id=1, replica_groups=mesh['head'=4,'ctx'=8] {'ctx'}, dimensions={0}, use_global_device_ids=true | all-gather | bytes 18432 | tf_op jit(solution)/shard_map/all_gather | solution.py:12
  198.3 30.9 %all_gather.30 = f32[8,2,2,16,8]{3,4,2,1,0:T(8,128)S(1)} all-gather(f32[1,2,2,16,8]{3,4,2,1,0:T(8,128)S(1)} %copy.83), channel_id=1, replica_groups=mesh['head'=4,'ctx'=8] {'ctx'}, dimensions={0}, use_global_device_ids=true | all-gather | bytes 18432 | tf_op jit(solution)/shard_map/all_gather | solution.py:12
  229.3 1.0 slice_bitcast_fusion
  230.3 9.9 %while.34 = (s32[]{:T(128)}, f32[2,2,16,8]{2,3,1,0:T(8,128)S(1)}, f32[2,2,16,8]{2,3,1,0:T(8,128)S(1)}, f32[2,2,16,8,128]{4,3,2,1,0:T(8,128)S(1)}, f32[8,2,2,16,8...) while((s32[]{:T(128)}, f32[2,2,16,8]{2,3,1,0:T(8,128)S(1)}, ...), condition=%wide.region_12.13_spmd, body=%wide.region_11.12_spmd.sunk | while | flops 199685 | bytes 815247 | solution.py:17
  230.3 0.1 copy.149
  230.5 1.2 fusion.64
  231.7 0.1 copy.149
  231.9 1.2 fusion.64
  233.1 0.1 copy.149
  233.2 0.1 copy.150
  233.3 1.2 fusion.64
  234.7 1.2 fusion.64
  236.1 1.2 fusion.64
  237.4 0.1 copy.149
  237.5 1.2 fusion.64
  238.8 0.1 copy.149
  238.9 1.2 fusion.64
  240.2 0.1 divide_convert_fusion
  240.5 5.6 %fusion.14 = bf16[16,2,2048]{2,0,1:T(8,128)(2,1)} fusion(bf16[2,2,16,1024]{3,2,1,0:T(8,128)(2,1)S(1)} %reshape.165, bf16[2,1024,2048,1]{2,1,3,0:T(8,128)(2,1)} %bitcast.136), kind=kOutput, calls=%fused_computation.24 | convolution fusion | flops 268500992 | bytes 8650752 | tf_op jit(solution)/shard_map/lmie,len->imn/dot_general | solution.py:194
  246.1 0.6 dynamic-slice
  247.3 30.8 %all-reduce.6.cloned.1.call-done = bf16[16,2,2048]{2,0,1:T(8,128)(2,1)} async-done(((bf16[16,2,2048]{2,0,1:T(8,128)(2,1)}), bf16[16,2,2048]{2,0,1:T(8,128)(2,1)}) %all-reduce.6.cloned.1.call-update) | async-done | bytes 131088
  278.1 0.9 constant_dynamic-slice_fusion.4
  279.0 0.6 copy.93
  (62 shorter events, 1.6 us)
Async XLA Ops:
  6.5 158.7 %copy-start = (bf16[2,128,2,128]{3,2,1,0:T(2,128)(2,1)S(1)}, bf16[2,128,2,128]{3,2,1,0:T(2,128)(2,1)}, u32[]{:S(2)}) copy-start(bf16[2,128,2,128]{3,2,1,0:T(2,128)(2,1)} %param.22) | copy-start | bytes 393220
  6.5 79.1 %all-reduce.4.cloned.1.call-start = ((), (), s32[]{:S(2)}) async-start(), calls=%async_computation.1 | async-start | bytes 524288 | tf_op jit(solution)/shard_map/psum | solution.py:64
  10.8 110.4 %reduce-scatter.3.cloned.1.call-start = ((), (), s32[]{:S(2)}) async-start(), calls=%async_computation.2 | async-start | bytes 327680 | tf_op jit(solution)/shard_map/reduce_scatter | solution.py:82
  101.6 127.7 %all-gather.2.cloned.1.call-start = ((), (), s32[]{:S(2)}) async-start(), calls=%async_computation.3 | async-start | bytes 2359296 | tf_op jit(solution)/shard_map/all_gather | solution.py:12
  155.4 10.6 %copy-start.2 = (bf16[2,128,2,128]{3,2,1,0:T(2,128)(2,1)S(1)}, bf16[2,128,2,128]{3,2,1,0:T(2,128)(2,1)}, u32[]{:S(2)}) copy-start(bf16[2,128,2,128]{3,2,1,0:T(2,128)(2,1)} %param.23) | copy-start | bytes 393220
  166.3 0.7 copy-start.1
  167.1 111.0 %all-reduce.6.cloned.1.call-start = ((), (), s32[]{:S(2)}) async-start(), calls=%async_computation.4 | async-start | bytes 262144
  240.5 5.6 %copy-start.3 = (u32[32]{0:T(128)S(1)}, u32[32]{0:T(128)}, u32[]{:S(2)}) copy-start(u32[32]{0:T(128)} %constant.135) | copy-start | bytes 388
Sparse Core Ops, SparseCore 0:
  11.0 74.6 all-reduce.3
  101.7 19.4 reduce-scatter.2
  167.2 50.6 all-gather.1
  246.2 31.8 all-reduce.5
where the time goes:
time: 287 us; the launch traced here: 286 us
  waiting for transfers between devices  123 us (43%)
  blocking collectives  99.4 us (35%)
  matrix products  22.4 us (8%)
  other arithmetic  16.7 us (6%)
  between operations  14.1 us (5%)
  local copies, waits for them, and re-layouts  9.88 us (3%)
    psum x1, waiting for transfers between devices, lookup_rows(): return lax.psum(picked, 'ctx').astype(jnp.float32).astype(jnp.bfloat16)  73.2 us
    all_gather x2, blocking collectives, combined_all(): gathered = jax.tree.map(lambda a: lax.all_gather(a, axis), part)  61.8 us
    all_gather x1, blocking collectives, project(): lax.all_gather(summed.astype(jnp.bfloat16), 'ctx', axis=2, tiled=True)  32 us
    unnamed x5, waiting for transfers between devices  30.8 us
    reduce_scatter x1, waiting for transfers between devices, project(): lax.psum_scatter(partial_summand(jnp.int32(0), lax.axis_size('head') * lo...  19.3 us
    add x7, other arithmetic, combine(): earlier[2] * first_scale[..., None] + later[2] * second_scale[..., None]  8.5 us
    dot_general x1, matrix products, partial_summand(): jnp.einsum('rd,dgf->grf', flattened_rows, qkv_weight, preferred_element_t...  8.08 us
  transfers between devices with their start and end apart: 4, of which 3 were waited for; matrix products, arithmetic and copies ran while one was open for 1% of the time, Pallas kernels for 0%

commit v1 on v0

--- a/solution.py
+++ b/solution.py
@@ -61,7 +61,7 @@
     inside_range = (offsets >= 0) & (offsets < local_rows)
     picked = jnp.take(embedding, jnp.clip(offsets, 0, local_rows - 1), axis=0)
     picked = jnp.where(inside_range[..., None], picked, jnp.zeros((), jnp.bfloat16))
-    return lax.psum(picked, "ctx").astype(jnp.float32).astype(jnp.bfloat16)
+    return jnp.sum(lax.all_gather(picked, "ctx"), axis=0).astype(jnp.float32).astype(jnp.bfloat16)
 
 
 def project(embedded, attn_gain, qkv_weight):

time: 287 us -> 265 us (0.923)
  waiting for transfers between devices: 123 us -> 101 us
    psum x1 -> x0, waiting for transfers between devices: 73.2 us -> none  [lookup_rows(): return lax.psum(picked, 'ctx').astype(jnp.float32).astype(jnp.bfloat16)]
    all_gather x0 -> x1, waiting for transfers between devices: none -> 51.2 us  [lookup_rows(): lax.all_gather(picked, 'ctx')]
where the time goes in v1:
time: 265 us; the launch traced here: 264 us
  waiting for transfers between devices  101 us (38%)
  blocking collectives  99.5 us (38%)
  matrix products  22.4 us (8%)
  other arithmetic  16.7 us (6%)
  between operations  14.1 us (5%)
  local copies, waits for them, and re-layouts  9.97 us (4%)
    all_gather x2, blocking collectives, combined_all(): gathered = jax.tree.map(lambda a: lax.all_gather(a, axis), part)  61.8 us
    all_gather x1, waiting for transfers between devices, lookup_rows(): lax.all_gather(picked, 'ctx')  51.2 us
    all_gather x1, blocking collectives, project(): lax.all_gather(summed.astype(jnp.bfloat16), 'ctx', axis=2, tiled=True)  32.1 us
    unnamed x5, waiting for transfers between devices  31 us
    reduce_scatter x1, waiting for transfers between devices, project(): lax.psum_scatter(partial_summand(jnp.int32(0), lax.axis_size('head') * lo...  18.6 us
    add x7, other arithmetic, combine(): earlier[2] * first_scale[..., None] + later[2] * second_scale[..., None]  8.49 us
    dot_general x1, matrix products, partial_summand(): jnp.einsum('rd,dgf->grf', flattened_rows, qkv_weight, preferred_element_t...  8.09 us
    psum x1, blocking collectives, project(): square_sum = lax.psum(jnp.sum(features * features, axis=-1), 'head')  5.65 us
  transfers between devices with their start and end apart: 4, of which 3 were waited for; matrix products, arithmetic and copies ran while one was open for 1% of the time, Pallas kernels for 0%

profile of v1, /device:TPU:0, one launch (start us, length us, event | category | flops | bytes accessed | tf_op | source)
XLA Modules:
  0.0 263.9 jit_solution(13602989719900700741)
XLA Ops:
  6.5 0.7 compare_and_fusion
  7.3 0.1 reshape.183
  7.4 2.7 %gather_fusion = bf16[32,4096]{1,0:T(8,128)(2,1)S(1)} fusion(bf16[8016,4096]{1,0:T(8,128)(2,1)} %param.16, s32[1024]{0:T(1024)S(1)} %pad_clamp_fusion), kind=kCustom, calls=%fused_computation | custom fusion | bytes 524416 | tf_op jit(solution)/shard_map/jit(_take)/gather | solution.py:62
  10.0 0.8 select_select_fusion
  11.0 0.7 dynamic_slice.74
  11.7 0.7 broadcast_add_fusion
  12.4 0.1 iota_compare_fusion.1
  12.5 51.2 %all-gather.3.cloned.1.call-done = bf16[8,2,16,4096]{3,2,1,0:T(8,128)(2,1)} async-done(((bf16[1,2,16,4096]{3,2,1,0:T(8,128)(2,1)}), bf16[8,2,16,4096]{3,2,1,0:T(8,128)(2,1)}) %all-gather.3.cloned.1.call-update) | async-done | bytes 2097168 | tf_op jit(solution)/shard_map/all_gather | solution.py:64
  63.7 1.9 reduce_sum.39
  65.7 0.1 multiply_reduce_fusion
  65.8 5.7 %psum.7 = f32[2,16]{1,0:T(2,128)S(1)} all-reduce(f32[2,16]{1,0:T(2,128)S(1)} %multiply_reduce_fusion), channel_id=1, replica_groups=mesh['head'=4,'ctx'=8] {'head'}, use_global_device_ids=true, to_apply=%region_2.3 | all-reduce | flops 32 | bytes 256 | tf_op jit(solution)/shard_map/psum | solution.py:69
  71.5 0.1 mul.232
  71.5 0.1 fusion.22
  71.7 8.1 %convolution_bitcast_fusion.2 = f32[8,32,160]{2,1,0:T(8,128)} fusion(bf16[4096,8,160]{0,2,1:T(8,128)(2,1)} %param.18, bf16[32,4096]{1,0:T(8,128)(2,1)S(1)} %fusion.22), kind=kOutput, calls=%fused_computation.25 | convolution fusion | flops 335544320 | bytes 10911744 | tf_op jit(solution)/shard_map/rd,dgf->grf/dot_general | solution.py:78
  79.9 0.3 multiply_cosine_fusion
  80.2 18.6 %reduce-scatter.3.cloned.1.call-done = f32[2,32,160]{2,1,0:T(8,128)} async-done(((f32[8,32,160]{2,1,0:T(8,128)}), f32[2,32,160]{2,1,0:T(8,128)}) %reduce-scatter.3.cloned.1.call-update) | async-done | bytes 40976 | tf_op jit(solution)/shard_map/reduce_scatter | solution.py:82
  98.8 0.8 convert_element_type.84
  99.6 0.1 copy.73
  99.7 32.1 %all_gather.32 = bf16[2,32,1280]{1,0,2:T(2,128)(2,1)S(1)} all-gather(bf16[2,32,160]{1,0,2:T(2,128)(2,1)S(1)} %copy.73), channel_id=1, replica_groups=mesh['head'=4,'ctx'=8] {'ctx'}, dimensions={2}, use_global_device_ids=true | all-gather | bytes 184320 | tf_op jit(solution)/shard_map/all_gather | solution.py:88
  131.8 0.4 copy.74
  132.3 0.1 fusion.42
  132.6 0.1 fusion.31
  132.7 0.1 add_convert_fusion
  132.8 0.1 fusion.23
  133.0 9.6 %while.33 = (s32[]{:T(128)}, f32[2,256]{1,0:T(2,128)S(1)}, f32[2,256]{1,0:T(2,128)S(1)}, f32[2,256,128]{2,1,0:T(8,128)S(1)}, bf16[2,256,128]{2,1,0:T(8,128)(2,1)...) while((s32[]{:T(128)}, f32[2,256]{1,0:T(2,128)S(1)}, ...), condition=%wide.region_7.8_spmd, body=%wide.region_4.7_spmd.sunk | while | flops 542113280 | bytes 14885997 | solution.py:101
  133.0 2.0 fusion.60
  135.1 0.8 convert_reduce_fusion.3
  135.9 1.9 fusion.61
  137.8 2.0 fusion.60
  139.9 0.8 convert_reduce_fusion.3
  140.7 1.9 fusion.61
  142.6 0.1 reshape.174
  142.8 0.1 reshape.175
  142.9 0.2 fusion.44
  143.1 0.3 fusion.45
  143.4 0.2 convert_reduce_fusion.1
  143.6 0.1 convolution_bitcast_fusion.4
  143.8 0.1 fusion.18
  143.9 0.7 copy-done.1
  144.7 0.1 all_gather.33
  144.8 0.1 all_gather.36
  145.0 0.1 copy.86
  145.1 30.8 %all_gather.38 = f32[8,2,2,16,8]{3,4,2,1,0:T(8,128)S(1)} all-gather(f32[1,2,2,16,8]{3,4,2,1,0:T(8,128)S(1)} %copy.86), channel_id=1, replica_groups=mesh['head'=4,'ctx'=8] {'ctx'}, dimensions={0}, use_global_device_ids=true | all-gather | bytes 18432 | tf_op jit(solution)/shard_map/all_gather | solution.py:12
  175.9 30.9 %all_gather.35 = f32[8,2,2,16,8]{3,4,2,1,0:T(8,128)S(1)} all-gather(f32[1,2,2,16,8]{3,4,2,1,0:T(8,128)S(1)} %copy.83), channel_id=1, replica_groups=mesh['head'=4,'ctx'=8] {'ctx'}, dimensions={0}, use_global_device_ids=true | all-gather | bytes 18432 | tf_op jit(solution)/shard_map/all_gather | solution.py:12
  206.9 1.0 slice_bitcast_fusion
  207.9 9.9 %while.34 = (s32[]{:T(128)}, f32[2,2,16,8]{2,3,1,0:T(8,128)S(1)}, f32[2,2,16,8]{2,3,1,0:T(8,128)S(1)}, f32[2,2,16,8,128]{4,3,2,1,0:T(8,128)S(1)}, f32[8,2,2,16,8...) while((s32[]{:T(128)}, f32[2,2,16,8]{2,3,1,0:T(8,128)S(1)}, ...), condition=%wide.region_12.13_spmd, body=%wide.region_11.12_spmd.sunk | while | flops 199685 | bytes 815247 | solution.py:17
  207.9 0.1 copy.149
  208.1 1.2 fusion.63
  209.5 1.2 fusion.63
  210.8 0.1 copy.149
  210.9 1.2 fusion.63
  212.2 0.1 copy.149
  212.3 1.2 fusion.63
  213.6 0.1 copy.149
  213.7 0.1 copy.150
  213.7 1.2 fusion.63
  215.1 1.2 fusion.63
  216.6 1.2 fusion.63
  217.9 0.1 divide_convert_fusion
  218.1 5.6 %fusion.14 = bf16[16,2,2048]{2,0,1:T(8,128)(2,1)} fusion(bf16[2,2,16,1024]{3,2,1,0:T(8,128)(2,1)S(1)} %reshape.177, bf16[2,1024,2048,1]{2,1,3,0:T(8,128)(2,1)} %bitcast.141), kind=kOutput, calls=%fused_computation.24 | convolution fusion | flops 268500992 | bytes 8650752 | tf_op jit(solution)/shard_map/lmie,len->imn/dot_general | solution.py:194
  223.7 0.6 dynamic-slice
  224.9 31.0 %all-reduce.3.cloned.1.call-done = bf16[16,2,2048]{2,0,1:T(8,128)(2,1)} async-done(((bf16[16,2,2048]{2,0,1:T(8,128)(2,1)}), bf16[16,2,2048]{2,0,1:T(8,128)(2,1)}) %all-reduce.3.cloned.1.call-update) | async-done | bytes 131088
  255.9 0.9 constant_dynamic-slice_fusion.4
  256.8 0.6 copy.93
  (66 shorter events, 1.8 us)
Async XLA Ops:
  6.5 136.3 %copy-start = (bf16[2,128,2,128]{3,2,1,0:T(2,128)(2,1)S(1)}, bf16[2,128,2,128]{3,2,1,0:T(2,128)(2,1)}, u32[]{:S(2)}) copy-start(bf16[2,128,2,128]{3,2,1,0:T(2,128)(2,1)} %param.22) | copy-start | bytes 393220
  6.5 65.0 %copy-start.3 = (f32[4096]{0:T(1024)S(1)}, f32[4096]{0:T(1024)}, u32[]{:S(2)}) copy-start(f32[4096]{0:T(1024)} %param.17) | copy-start | bytes 49156
  6.5 57.2 %all-gather.3.cloned.1.call-start = ((), (), s32[]{:S(2)}) async-start(), calls=%async_computation.1 | async-start | bytes 2359296 | tf_op jit(solution)/shard_map/all_gather | solution.py:64
  10.9 87.9 %reduce-scatter.3.cloned.1.call-start = ((), (), s32[]{:S(2)}) async-start(), calls=%async_computation.2 | async-start | bytes 327680 | tf_op jit(solution)/shard_map/reduce_scatter | solution.py:82
  79.8 127.1 %all-gather.5.cloned.1.call-start = ((), (), s32[]{:S(2)}) async-start(), calls=%async_computation.3 | async-start | bytes 2359296 | tf_op jit(solution)/shard_map/all_gather | solution.py:12
  133.0 10.6 %copy-start.2 = (bf16[2,128,2,128]{3,2,1,0:T(2,128)(2,1)S(1)}, bf16[2,128,2,128]{3,2,1,0:T(2,128)(2,1)}, u32[]{:S(2)}) copy-start(bf16[2,128,2,128]{3,2,1,0:T(2,128)(2,1)} %param.23) | copy-start | bytes 393220
  143.9 0.7 copy-start.1
  144.7 111.2 %all-reduce.3.cloned.1.call-start = ((), (), s32[]{:S(2)}) async-start(), calls=%async_computation.4 | async-start | bytes 262144
  218.1 5.6 %copy-start.4 = (u32[32]{0:T(128)S(1)}, u32[32]{0:T(128)}, u32[]{:S(2)}) copy-start(u32[32]{0:T(128)} %constant.136) | copy-start | bytes 388
Sparse Core Ops, SparseCore 0:
  11.0 52.7 all-gather.2
  79.9 18.7 reduce-scatter.2
  144.8 50.5 all-gather.4
  223.8 32.0 all-reduce.2
